TPU v7x, 32 devices: a 4x2x2 block of a 4x4x8 slice. The times are simulated.
32 devices in a mesh: dp: 4 (over y, z), sp: 8 (over x, core).
Axes of the slice: x: 4, y: 2, z: 2, core: 2. Of those that a mesh axis runs over, the one named last changes fastest.
The devices are a block of a 4x4x8 slice.
Arguments:
- latents: bfloat16 [32, 16, 64, 1280], P('dp', 'sp'), parts along dimension 0
- time_emb: bfloat16 [32, 1280], P('dp'), parts along dimension 0
- context: bfloat16 [32, 77, 768], P('dp'), parts along dimension 0
- res_norm: float32 [2, 2, 2, 1280], replicated
- res_conv_w: bfloat16 [2, 2, 3, 3, 1280, 1280], replicated
- res_conv_b: float32 [2, 2, 1280], replicated
- res_temb_w: bfloat16 [2, 1280, 1280], replicated
- res_temb_b: float32 [2, 1280], replicated
- tr_norm: float32 [2, 1280], replicated
- proj_w: bfloat16 [2, 1280, 1280], replicated
- proj_b: float32 [2, 1280], replicated
- ln_par: float32 [2, 3, 2, 1280], replicated
- self_qkv: bfloat16 [2, 3, 1280, 8, 160], replicated
- cross_q: bfloat16 [2, 1280, 8, 160], replicated
- cross_kv: bfloat16 [2, 2, 768, 8, 160], replicated
- attn_out: bfloat16 [2, 2, 8, 160, 1280], replicated
- attn_b: float32 [2, 2, 1280], replicated
- ff_in_w: bfloat16 [2, 1280, 10240], replicated
- ff_in_b: float32 [2, 10240], replicated
- ff_out_w: bfloat16 [2, 5120, 1280], replicated
- ff_out_b: float32 [2, 1280], replicated
Outputs:
- output: bfloat16 [32, 16, 64, 1280], P('dp', 'sp'), parts along dimension 0
There are 4 independent parts. A program takes and returns all parts, laid end to end along the dimension named above; an argument that names none is the same for every part.
All inputs are finite; a program needn't handle non-finite values.
Results may differ from a plain program's by a relative error of at most 0.0196095.
Values are sent between devices in bfloat16 or wider.
A program may use at most 768 MiB of HBM per device.

v0:
```python
import functools
import math
import jax
import jax.numpy as jnp
from jax import lax
from jax.sharding import PartitionSpec as P

NUM_GROUPS = 32


def group_norm_sp(values, norm_gain, norm_bias, eps_val, sp_size):
    batch_n, rows_n, cols_n, chan_n = values.shape
    grouped = values.astype(jnp.float32).reshape(batch_n, rows_n, cols_n, NUM_GROUPS, chan_n // NUM_GROUPS)
    local_sums = jnp.stack([grouped.sum(axis=(1, 2, 4)), (grouped * grouped).sum(axis=(1, 2, 4))])
    total_sums = lax.psum(local_sums, 'sp')
    count_n = rows_n * sp_size * cols_n * (chan_n // NUM_GROUPS)
    grp_mean = total_sums[0] / count_n
    grp_var = total_sums[1] / count_n - grp_mean * grp_mean
    inv_std = lax.rsqrt(grp_var + eps_val)
    normed = (grouped - grp_mean[:, None, None, :, None]) * inv_std[:, None, None, :, None]
    return normed.reshape(batch_n, rows_n, cols_n, chan_n) * norm_gain + norm_bias


def conv_rows(act_in, kernel, sp_size):
    to_next = [(position, position + 1) for position in range(sp_size - 1)]
    to_prev = [(position + 1, position) for position in range(sp_size - 1)]
    from_above = lax.ppermute(act_in[:, -1:], 'sp', to_next)
    from_below = lax.ppermute(act_in[:, :1], 'sp', to_prev)
    padded = jnp.concatenate([from_above, act_in, from_below], axis=1)
    return lax.conv_general_dilated(padded, kernel, (1, 1), ((0, 0), (1, 1)), dimension_numbers=('NHWC', 'HWIO', 'NHWC'), preferred_element_type=jnp.float32)


def resnet_local(latents, time_emb, res_index, res_norm, res_conv_w, res_conv_b, res_temb_w, res_temb_b, sp_size):
    first_act = jax.nn.silu(group_norm_sp(latents, res_norm[res_index, 0, 0], res_norm[res_index, 0, 1], 1e-5, sp_size)).astype(jnp.bfloat16)
    time_proj = jnp.dot(jax.nn.silu(time_emb.astype(jnp.float32)).astype(jnp.bfloat16), res_temb_w[res_index], preferred_element_type=jnp.float32) + res_temb_b[res_index]
    hidden = (conv_rows(first_act, res_conv_w[res_index, 0], sp_size) + res_conv_b[res_index, 0] + time_proj[:, None, None, :]).astype(jnp.bfloat16)
    second_act = jax.nn.silu(group_norm_sp(hidden, res_norm[res_index, 1, 0], res_norm[res_index, 1, 1], 1e-5, sp_size)).astype(jnp.bfloat16)
    update = conv_rows(second_act, res_conv_w[res_index, 1], sp_size) + res_conv_b[res_index, 1]
    return (latents.astype(jnp.float32) + update).astype(jnp.bfloat16)


def layer_norm(values, norm_gain, norm_bias):
    centered = values.astype(jnp.float32)
    centered = centered - centered.mean(axis=-1, keepdims=True)
    variance = (centered * centered).mean(axis=-1, keepdims=True)
    return (centered * lax.rsqrt(variance + 1e-5) * norm_gain + norm_bias).astype(jnp.bfloat16)


def attend_block(q_blk, k_all, v_all):
    scale_f = 1.0 / math.sqrt(q_blk.shape[-1])
    scores = jnp.einsum('bqhd,bkhd->bhqk', q_blk, k_all, preferred_element_type=jnp.float32) * scale_f
    row_exp = jnp.exp(scores - scores.max(axis=-1, keepdims=True))
    row_sum = row_exp.sum(axis=-1)
    row_out = jnp.einsum('bhqk,bkhd->bqhd', row_exp.astype(jnp.bfloat16), v_all, preferred_element_type=jnp.float32)
    return (row_out / jnp.swapaxes(row_sum, 1, 2)[..., None]).astype(jnp.bfloat16)


def attend_rows(q_all, k_all, v_all, rows_n):
    batch_n, tok_n, head_n, dim_n = q_all.shape
    q_rows = jnp.swapaxes(q_all.reshape(batch_n, rows_n, tok_n // rows_n, head_n, dim_n), 0, 1)
    attended = lax.map(lambda q_row: attend_block(q_row, k_all, v_all), q_rows)
    return jnp.swapaxes(attended, 0, 1).reshape(batch_n, tok_n, head_n, dim_n)


def transformer_local(hidden, context, tr_norm, proj_w, proj_b, ln_par, self_qkv, cross_q, cross_kv, attn_out, attn_b, ff_in_w, ff_in_b, ff_out_w, ff_out_b, sp_size):
    batch_n, rows_n, cols_n, chan_n = hidden.shape
    normed = group_norm_sp(hidden, tr_norm[0], tr_norm[1], 1e-6, sp_size).astype(jnp.bfloat16).reshape(batch_n, rows_n * cols_n, chan_n)
    hidden_tok = (jnp.einsum('bnc,cd->bnd', normed, proj_w[0], preferred_element_type=jnp.float32) + proj_b[0]).astype(jnp.bfloat16)
    ff_width = ff_out_w.shape[1]
    for layer_i in range(ln_par.shape[0]):
        normed = layer_norm(hidden_tok, ln_par[layer_i, 0, 0], ln_par[layer_i, 0, 1])
        qkv_loc = jnp.einsum('bnc,jchd->jbnhd', normed, self_qkv[layer_i], preferred_element_type=jnp.float32).astype(jnp.bfloat16)
        qkv_heads = lax.all_to_all(qkv_loc, 'sp', 3, 2, tiled=True)
        attended = attend_rows(qkv_heads[0], qkv_heads[1], qkv_heads[2], rows_n * sp_size)
        att_rows = lax.all_to_all(attended, 'sp', 1, 2, tiled=True)
        hidden_tok = (hidden_tok.astype(jnp.float32) + jnp.einsum('bnhd,hdc->bnc', att_rows, attn_out[layer_i, 0], preferred_element_type=jnp.float32) + attn_b[layer_i, 0]).astype(jnp.bfloat16)
        normed = layer_norm(hidden_tok, ln_par[layer_i, 1, 0], ln_par[layer_i, 1, 1])
        q_cross = jnp.einsum('bnc,chd->bnhd', normed, cross_q[layer_i], preferred_element_type=jnp.float32).astype(jnp.bfloat16)
        kv_cross = jnp.einsum('btc,jchd->jbthd', context, cross_kv[layer_i], preferred_element_type=jnp.float32).astype(jnp.bfloat16)
        crossed = attend_block(q_cross, kv_cross[0], kv_cross[1])
        hidden_tok = (hidden_tok.astype(jnp.float32) + jnp.einsum('bnhd,hdc->bnc', crossed, attn_out[layer_i, 1], preferred_element_type=jnp.float32) + attn_b[layer_i, 1]).astype(jnp.bfloat16)
        normed = layer_norm(hidden_tok, ln_par[layer_i, 2, 0], ln_par[layer_i, 2, 1])
        ff_proj = jnp.einsum('bnc,cf->bnf', normed, ff_in_w[layer_i], preferred_element_type=jnp.float32) + ff_in_b[layer_i]
        gated_act = (ff_proj[..., :ff_width] * jax.nn.gelu(ff_proj[..., ff_width:], approximate=False)).astype(jnp.bfloat16)
        hidden_tok = (hidden_tok.astype(jnp.float32) + jnp.einsum('bnf,fc->bnc', gated_act, ff_out_w[layer_i], preferred_element_type=jnp.float32) + ff_out_b[layer_i]).astype(jnp.bfloat16)
    out_tok = jnp.einsum('bnc,cd->bnd', hidden_tok, proj_w[1], preferred_element_type=jnp.float32) + proj_b[1] + hidden.reshape(batch_n, rows_n * cols_n, chan_n).astype(jnp.float32)
    return out_tok.astype(jnp.bfloat16).reshape(batch_n, rows_n, cols_n, chan_n)


def device_block(latents, time_emb, context, res_norm, res_conv_w, res_conv_b, res_temb_w, res_temb_b, tr_norm, proj_w, proj_b, ln_par, self_qkv, cross_q, cross_kv, attn_out, attn_b, ff_in_w, ff_in_b, ff_out_w, ff_out_b, sp_size):
    first_out = resnet_local(latents, time_emb, 0, res_norm, res_conv_w, res_conv_b, res_temb_w, res_temb_b, sp_size)
    middle = transformer_local(first_out, context, tr_norm, proj_w, proj_b, ln_par, self_qkv, cross_q, cross_kv, attn_out, attn_b, ff_in_w, ff_in_b, ff_out_w, ff_out_b, sp_size)
    return resnet_local(middle, time_emb, 1, res_norm, res_conv_w, res_conv_b, res_temb_w, res_temb_b, sp_size)


def solution(mesh):
    sp_size = mesh.shape['sp']
    row_spec = P('dp', 'sp')
    part_spec = P('dp')
    in_specs = (row_spec, part_spec, part_spec) + (P(),) * 18
    body_fn = functools.partial(device_block, sp_size=sp_size)
    return jax.shard_map(body_fn, mesh=mesh, in_specs=in_specs, out_specs=row_spec, check_vma=False)
```

profile of v0, /device:TPU:81, one launch (start us, length us, event | category | flops | bytes accessed | tf_op | source)
XLA Modules:
  0.0 1223.9 jit_solution(1694981285672049474)
XLA Ops:
  3.7 14.1 %psum.35 = f32[2,8,32]{2,1,0:T(8,128)S(1)} all-reduce(f32[2,8,32]{2,1,0:T(8,128)S(1)} %pad_maximum_fusion), channel_id=1, replica_groups=mesh['dp'=4,'sp'=8] {'sp'}, use_global_device_ids=true, to_apply=%region_4.5 | all-reduce | flops 512 | bytes 4096 | tf_op jit(solution)/shard_map/psum | solution.py:15
  33.6 7.5 collective-permute-done
  45.6 34.9 %convert_reduce_fusion.8 = (f32[8,1280]{1,0:T(8,128)S(1)}, f32[8,1280]{1,0:T(8,128)S(1)}, bf16[8,2,64,1280]{3,0,2,1:T(8,128)(2,1)}) fusion(f32[8,1280]{1,0:T(8,128)S(1)} %fusion.352, f32[1280]{0:T(1024)S(1)} %get-tuple-element.123, bf16[2,2,3,3,1280,1280]{5,4,3,2,1,0:T(8,128)(2,1)} %param.29, bf16[8,1,64,1280]{3,0,2,1:T(8,128)(2,1)S(1)} %collective-permute-done.1, ...), kind=kOutput, calls=%fused_computation.139 | convolution fusion | flops 29909299200 | bytes 37483520 | tf_op jit(solution)/shard_map/conv_general_dilated | solution.py:30
  81.0 9.9 psum.36
  103.6 10.4 collective-permute-done.2
  118.5 35.5 %convert_reduce_fusion.9 = (f32[8,1280]{1,0:T(8,128)S(1)}, f32[8,1280]{1,0:T(8,128)S(1)}, bf16[8,2,64,1280]{3,0,2,1:T(8,128)(2,1)}) fusion(f32[1280]{0:T(1024)S(1)} %get-tuple-element.122, bf16[2,2,3,3,1280,1280]{5,4,3,2,1,0:T(8,128)(2,1)} %param.29, bf16[8,1,64,1280]{3,0,2,1:T(8,128)(2,1)S(1)} %collective-permute-done.3, ...), kind=kOutput, calls=%fused_computation.261 | convolution fusion | flops 29910609920 | bytes 40064000 | tf_op jit(solution)/shard_map/conv_general_dilated | solution.py:30
  154.4 9.9 psum.37
  167.6 6.2 convert_reduce_fusion.7
  175.3 13.7 %convert_bitcast_fusion.1 = bf16[3,8,128,8,160]{2,4,3,0,1:T(8,128)(2,1)S(1)} fusion(bf16[2,3,1280,8,160]{2,4,3,1,0:T(8,128)(2,1)} %param.37, bf16[8,128,1280]{2,1,0:T(8,128)(2,1)S(1)} %get-tuple-element.186, f32[1280]{0:T(1024)S(1)} %get-tuple-element.110, f32[1280]{0:T(1024)S(1)} %get-tuple-element.111, f32[8,128]{1,0:T(8,128)S(1)} %add_rsqrt_fusion.5, ...), kind=kOutput, calls=%fused_computation.133 | convolution fusion | flops 10078126080 | bytes 20334592 | tf_op jit(solution)/shard_map/bnc,jchd->jbnhd/dot_general | solution.py:72
  193.7 9.0 all-to-all-start
  202.7 6.2 convert_bitcast_fusion.3
  214.7 75.8 %all-to-all-done = bf16[3,8,128,8,160]{2,4,0,1,3:T(8,128)(2,1)} async-done(((bf16[3,8,128,8,160]{2,4,0,1,3:T(8,128)(2,1)}), bf16[3,8,128,8,160]{2,4,0,1,3:T(8,128)(2,1)}, u32[]{:S(2)}, u32[]{:S(2)}) %all-to-all-start) | async-done | bytes 7864352 | tf_op jit(solution)/shard_map/all_to_all | solution.py:73
  298.8 7.5 reshape_squeeze.6
  306.3 8.2 copy.87
  337.2 78.7 %while.20 = (s32[]{:T(128)}, bf16[16,8,64,1,160]{4,2,1,3,0:T(8,128)(2,1)}, bf16[16,8,64,1,160]{4,2,1,3,0:T(8,128)(2,1)}, bf16[8,1024,1,160]{1,3,0,2:T(8,128)(2,1)}, bf16[8,1024,1,160]{1,3,0,2:T(8,128)(2,1)}, /*index=5*/s32[]{:T(128)}) while((s32[]{:T(128)}, bf16[16,8,64,1,160]{4,2,1,3,0:T(8,128)(2,1)}, ...), condition=%wide.region_20.21_spmd, body=%wide.region_17.20_spmd.sunk | while | flops 339901440 | bytes 22555744 | solution.py:61
  415.9 7.0 copy.124
  423.0 5.6 all-to-all-start.1
  429.9 47.3 %all-to-all-done.1 = bf16[8,1024,1,160]{3,0,2,1:T(8,128)(2,1)} async-done(((bf16[8,1024,1,160]{3,0,2,1:T(8,128)(2,1)}), bf16[8,1024,1,160]{3,0,2,1:T(8,128)(2,1)}, u32[]{:S(2)}, u32[]{:S(2)}) %all-to-all-start.1) | async-done | bytes 2621472 | tf_op jit(solution)/shard_map/all_to_all | solution.py:75
  477.2 8.6 copy.125
  485.8 8.0 convert_reduce_fusion.6
  496.2 8.7 multiply_reduce_fusion.5
  507.2 9.5 convert_reduce_fusion.5
  519.4 38.1 %fusion.90 = f32[8,128,10240]{2,1,0:T(8,128)} fusion(bf16[2,1280,10240]{2,1,0:T(8,128)(2,1)} %param.42, f32[10240]{0:T(1024)S(1)} %bitcast.489, bf16[8,128,1280]{2,1,0:T(8,128)(2,1)} %get-tuple-element.192, f32[1280]{0:T(1024)S(1)} %copy-done.33, f32[1280]{0:T(1024)S(1)} %copy-done.34, f32[8,128]{1,0:T(8,128)S(1)} %add_rsqrt_fusion.3, ...), kind=kOutput, calls=%fused_computation.58 | convolution fusion | flops 26861895680 | bytes 70838272 | tf_op jit(solution)/shard_map/bnc,cf->bnf/dot_general | solution.py:83
  557.4 64.6 %convert_reduce_fusion.4 = (f32[8,128]{1,0:T(8,128)S(1)}, bf16[8,128,1280]{2,1,0:T(8,128)(2,1)S(1)}) fusion(f32[1280]{0:T(1024)S(1)} %copy-done.42, bf16[2,5120,1280]{2,1,0:T(8,128)(2,1)} %param.44, f32[8,128,10240]{2,1,0:T(8,128)} %fusion.90, bf16[8,128,1280]{2,1,0:T(8,128)(2,1)S(1)} %copy-done.12), kind=kOutput, calls=%fused_computation.126 | convolution fusion | flops 13775666176 | bytes 60302336 | tf_op jit(solution)/shard_map/bnf,fc->bnc/dot_general | solution.py:85
  623.6 15.0 %convert_bitcast_fusion = bf16[3,8,128,8,160]{2,4,3,0,1:T(8,128)(2,1)} fusion(bf16[2,3,1280,8,160]{2,4,3,1,0:T(8,128)(2,1)} %param.37, bf16[8,128,1280]{2,1,0:T(8,128)(2,1)S(1)} %get-tuple-element.194, f32[1280]{0:T(1024)S(1)} %copy-done.31, f32[1280]{0:T(1024)S(1)} %copy-done.32, f32[8,128]{1,0:T(8,128)S(1)} %add_rsqrt_fusion.2, ...), kind=kOutput, calls=%fused_computation.123 | convolution fusion | flops 10078126080 | bytes 20334592 | tf_op jit(solution)/shard_map/bnc,jchd->jbnhd/dot_general | solution.py:72
  643.4 91.9 %all_to_all.66 = bf16[3,8,128,8,160]{2,4,0,1,3:T(8,128)(2,1)S(1)} all-to-all(bf16[3,8,128,8,160]{2,4,0,1,3:T(8,128)(2,1)S(1)} %copy.95), channel_id=1, replica_groups=mesh['dp'=4,'sp'=8] {'sp'}, dimensions={3} | all-to-all | bytes 15728640 | tf_op jit(solution)/shard_map/all_to_all | solution.py:73
  741.1 7.5 reshape_squeeze.7
  748.5 8.2 copy.99
  771.8 5.2 squeeze.120
  779.6 78.5 %while.21 = (s32[]{:T(128)}, bf16[16,8,64,1,160]{4,2,1,3,0:T(8,128)(2,1)}, bf16[16,8,64,1,160]{4,2,1,3,0:T(8,128)(2,1)}, bf16[8,1024,1,160]{1,3,0,2:T(8,128)(2,1)}, bf16[8,1024,1,160]{1,3,0,2:T(8,128)(2,1)}, /*index=5*/s32[]{:T(128)}) while((s32[]{:T(128)}, bf16[16,8,64,1,160]{4,2,1,3,0:T(8,128)(2,1)}, ...), condition=%wide.region_32.33_spmd, body=%wide.region_29.32_spmd.sunk | while | flops 339901440 | bytes 22555744 | solution.py:61
  858.2 7.0 copy.129
  865.2 5.9 all-to-all-start.3
  871.1 6.1 convert_bitcast_fusion.2
  882.8 36.8 %all-to-all-done.3 = bf16[8,1024,1,160]{3,0,2,1:T(8,128)(2,1)} async-done(((bf16[8,1024,1,160]{3,0,2,1:T(8,128)(2,1)}), bf16[8,1024,1,160]{3,0,2,1:T(8,128)(2,1)}, u32[]{:S(2)}, u32[]{:S(2)}) %all-to-all-start.3) | async-done | bytes 2621472 | tf_op jit(solution)/shard_map/all_to_all | solution.py:75
  919.6 8.5 copy.130
  928.2 8.0 convert_reduce_fusion.3
  938.6 9.1 multiply_reduce_fusion.4
  950.0 9.0 convert_reduce_fusion.2
  961.7 38.1 %fusion.93 = f32[8,128,10240]{2,1,0:T(8,128)} fusion(bf16[2,1280,10240]{2,1,0:T(8,128)(2,1)} %param.42, f32[10240]{0:T(1024)S(1)} %bitcast.488, bf16[8,128,1280]{2,1,0:T(8,128)(2,1)} %get-tuple-element.200, f32[1280]{0:T(1024)S(1)} %copy-done.28, f32[1280]{0:T(1024)S(1)} %copy-done.27, f32[8,128]{1,0:T(8,128)S(1)} %add_rsqrt_fusion, ...), kind=kOutput, calls=%fused_computation.59 | convolution fusion | flops 26861895680 | bytes 70838272 | tf_op jit(solution)/shard_map/bnc,cf->bnf/dot_general | solution.py:83
  999.8 64.7 %fusion.193.clone.1.clone.5 = bf16[8,128,1280]{2,1,0:T(8,128)(2,1)S(1)} fusion(bf16[8,128,1280]{2,1,0:T(8,128)(2,1)S(1)} %copy-done.13, bf16[2,5120,1280]{2,1,0:T(8,128)(2,1)} %param.44, f32[8,128,10240]{2,1,0:T(8,128)} %fusion.93, f32[1280]{0:T(1024)S(1)} %copy-done.41), kind=kOutput, calls=%fused_computation.197.clone.clone.clone.clone.clone.2 | convolution fusion | flops 13773045760 | bytes 60298240 | tf_op jit(solution)/shard_map/bnf,fc->bnc/dot_general | solution.py:85
  1064.5 6.4 fusion.521
  1071.4 13.2 %psum.38 = f32[2,8,32]{2,1,0:T(8,128)S(1)} all-reduce(f32[2,8,32]{2,1,0:T(8,128)S(1)} %pad_maximum_fusion.3), channel_id=1, replica_groups=mesh['dp'=4,'sp'=8] {'sp'}, use_global_device_ids=true, to_apply=%region_43.44 | all-reduce | flops 512 | bytes 4096 | tf_op jit(solution)/shard_map/psum | solution.py:15
  1085.1 5.5 copy.108
  1098.8 11.2 collective-permute-done.4
  1114.4 34.9 %convert_reduce_fusion.1 = (f32[8,1280]{1,0:T(8,128)S(1)}, f32[8,1280]{1,0:T(8,128)S(1)}, bf16[8,2,64,1280]{3,0,2,1:T(8,128)(2,1)}) fusion(f32[8,1280]{1,0:T(8,128)S(1)} %fusion.355, f32[1280]{0:T(1024)S(1)} %copy-done.39, bf16[2,2,3,3,1280,1280]{5,4,3,2,1,0:T(8,128)(2,1)} %param.29, bf16[8,1,64,1280]{3,0,2,1:T(8,128)(2,1)S(1)} %collective-permute-done.5, ...), kind=kOutput, calls=%fused_computation.116 | convolution fusion | flops 29909299200 | bytes 37483520 | tf_op jit(solution)/shard_map/conv_general_dilated | solution.py:30
  1149.9 9.7 psum.39
  1171.1 11.7 collective-permute-done.6
  1187.2 34.3 %add_convert_fusion = bf16[8,2,64,1280]{3,0,2,1:T(8,128)(2,1)S(1)} fusion(f32[8,2,64,1280]{3,0,2,1:T(8,128)S(1)} %bitcast.480, bf16[2,2,3,3,1280,1280]{5,4,3,2,1,0:T(8,128)(2,1)} %param.29, bf16[8,1,64,1280]{3,0,2,1:T(8,128)(2,1)S(1)} %collective-permute-done.7, bf16[8,2,64,1280]{3,0,2,1:T(8,128)(2,1)S(1)} %fusion.203, ...), kind=kOutput, calls=%fused_computation.245 | convolution fusion | flops 29904076800 | bytes 42603520 | tf_op jit(solution)/shard_map/conv_general_dilated | solution.py:30
  (398 shorter events, 327.2 us)
Async XLA Ops:
  0.0 202.7 %copy-start = (bf16[8,77,768]{2,0,1:T(8,128)(2,1)S(1)}, bf16[8,77,768]{2,0,1:T(8,128)(2,1)}, u32[]{:S(2)}) copy-start(bf16[8,77,768]{2,0,1:T(8,128)(2,1)} %param.27) | copy-start | bytes 2838532
  19.8 10.1 copy-start.23
  19.8 10.8 copy-start.21
  19.8 11.4 copy-start.46
  23.8 17.3 %collective-permute-start = (bf16[8,1,64,1280]{3,0,2,1:T(8,128)(2,1)S(1)}, bf16[8,1,64,1280]{3,0,2,1:T(8,128)(2,1)S(1)}, u32[]{:S(2)}, u32[]{:S(2)}) collective-permute-start(bf16[8,1,64,1280]{3,0,2,1:T(8,128)(2,1)S(1)} %get-tuple-element.179), channel_id=1, source_target_pairs={{0,1},{1,2},{2,3},{3,4},{4,5},{5,6},{6,7},{8,9},{9,10},{10,11},{11... | collective-permute-start | bytes 3932168 | tf_op jit(solution)/shard_map/ppermute | solution.py:27
  26.6 19.0 %collective-permute-start.1 = (bf16[8,1,64,1280]{3,0,2,1:T(8,128)(2,1)S(1)}, bf16[8,1,64,1280]{3,0,2,1:T(8,128)(2,1)S(1)}, u32[]{:S(2)}, u32[]{:S(2)}) collective-permute-start(bf16[8,1,64,1280]{3,0,2,1:T(8,128)(2,1)S(1)} %get-tuple-element.180), channel_id=1, source_target_pairs={{1,0},{2,1},{3,2},{4,3},{5,4},{6,5},{7,6},{9,8},{10,9},{11,10},{12... | collective-permute-start | bytes 3932168 | tf_op jit(solution)/shard_map/ppermute | solution.py:28
  91.3 10.8 copy-start.24
  91.4 10.8 copy-start.25
  91.4 10.8 copy-start.26
  91.4 11.4 copy-start.15
  91.4 27.1 %copy-start.3 = (bf16[8,2,64,1280]{3,2,1,0:T(8,128)(2,1)S(1)}, bf16[8,2,64,1280]{3,2,1,0:T(8,128)(2,1)}, u32[]{:S(2)}) copy-start(bf16[8,2,64,1280]{3,2,1,0:T(8,128)(2,1)} %param.25) | copy-start | bytes 7864324
  95.3 18.7 %collective-permute-start.2 = (bf16[8,1,64,1280]{3,0,2,1:T(8,128)(2,1)S(1)}, bf16[8,1,64,1280]{3,0,2,1:T(8,128)(2,1)S(1)}, u32[]{:S(2)}, u32[]{:S(2)}) collective-permute-start(bf16[8,1,64,1280]{3,0,2,1:T(8,128)(2,1)S(1)} %get-tuple-element.177), channel_id=1, source_target_pairs={{0,1},{1,2},{2,3},{3,4},{4,5},{5,6},{6,7},{8,9},{9,10},{10,11},{11... | collective-permute-start | bytes 3932168 | tf_op jit(solution)/shard_map/ppermute | solution.py:27
  99.5 19.0 %collective-permute-start.3 = (bf16[8,1,64,1280]{3,0,2,1:T(8,128)(2,1)S(1)}, bf16[8,1,64,1280]{3,0,2,1:T(8,128)(2,1)S(1)}, u32[]{:S(2)}, u32[]{:S(2)}) collective-permute-start(bf16[8,1,64,1280]{3,0,2,1:T(8,128)(2,1)S(1)} %get-tuple-element.178), channel_id=1, source_target_pairs={{1,0},{2,1},{3,2},{4,3},{5,4},{6,5},{7,6},{9,8},{10,9},{11,10},{12... | collective-permute-start | bytes 3932168 | tf_op jit(solution)/shard_map/ppermute | solution.py:28
  193.7 17.9 %slice-start.2 = ((s8[13107200]{0:T(1024)(128)(4,1)}), s8[524288]{0:T(1024)(128)(4,1)S(1)}, s32[]{:S(2)}) async-start(s8[13107200]{0:T(1024)(128)(4,1)} %bitcast.485), calls=%async_computation.6 | async-start | bytes 1048576
  193.7 96.8 %all-to-all-start = ((bf16[3,8,128,8,160]{2,4,0,1,3:T(8,128)(2,1)}), bf16[3,8,128,8,160]{2,4,0,1,3:T(8,128)(2,1)}, u32[]{:S(2)}, u32[]{:S(2)}) async-start(bf16[3,8,128,8,160]{2,4,0,1,3:T(8,128)(2,1)} %copy.83), calls=%async_computation | async-start | bytes 15728640 | tf_op jit(solution)/shard_map/all_to_all | solution.py:73
  423.0 54.2 %all-to-all-start.1 = ((bf16[8,1024,1,160]{3,0,2,1:T(8,128)(2,1)}), bf16[8,1024,1,160]{3,0,2,1:T(8,128)(2,1)}, u32[]{:S(2)}, u32[]{:S(2)}) async-start(bf16[8,1024,1,160]{3,0,2,1:T(8,128)(2,1)} %bitcast.483), calls=%async_computation.1 | async-start | bytes 8388608 | tf_op jit(solution)/shard_map/all_to_all | solution.py:75
  485.8 10.4 copy-start.35
  485.8 10.4 copy-start.36
  507.2 12.1 copy-start.33
  507.2 12.1 copy-start.34
  519.3 38.1 %copy-start.12 = (bf16[8,128,1280]{2,1,0:T(8,128)(2,1)S(1)}, bf16[8,128,1280]{2,1,0:T(8,128)(2,1)}, u32[]{:S(2)}) copy-start(bf16[8,128,1280]{2,1,0:T(8,128)(2,1)} %get-tuple-element.192) | copy-start | bytes 7864324
  519.3 38.1 %copy-start.42 = (f32[1280]{0:T(1024)S(1)}, f32[1280]{0:T(1024)}, u32[]{:S(2)}) copy-start(f32[1280]{0:T(1024)} %get-tuple-element.132) | copy-start | bytes 15364
  557.4 66.2 %copy-start.31 = (f32[1280]{0:T(1024)S(1)}, f32[1280]{0:T(1024)}, u32[]{:S(2)}) copy-start(f32[1280]{0:T(1024)} %get-tuple-element.104) | copy-start | bytes 15364
  557.4 66.2 %copy-start.32 = (f32[1280]{0:T(1024)S(1)}, f32[1280]{0:T(1024)}, u32[]{:S(2)}) copy-start(f32[1280]{0:T(1024)} %get-tuple-element.105) | copy-start | bytes 15364
  865.2 54.4 %all-to-all-start.3 = ((bf16[8,1024,1,160]{3,0,2,1:T(8,128)(2,1)}), bf16[8,1024,1,160]{3,0,2,1:T(8,128)(2,1)}, u32[]{:S(2)}, u32[]{:S(2)}) async-start(bf16[8,1024,1,160]{3,0,2,1:T(8,128)(2,1)} %bitcast.484), calls=%async_computation.3 | async-start | bytes 8388608 | tf_op jit(solution)/shard_map/all_to_all | solution.py:75
  882.8 45.3 %copy-start.44 = (f32[1280]{0:T(1024)S(1)}, f32[1280]{0:T(1024)}, u32[]{:S(2)}) copy-start(f32[1280]{0:T(1024)} %get-tuple-element.128) | copy-start | bytes 15364
  928.2 10.4 copy-start.29
  928.2 10.4 copy-start.30
  938.6 11.4 copy-start.43
  950.0 11.6 copy-start.16
  950.0 11.6 copy-start.27
  950.0 11.6 copy-start.28
  961.6 38.1 %copy-start.13 = (bf16[8,128,1280]{2,1,0:T(8,128)(2,1)S(1)}, bf16[8,128,1280]{2,1,0:T(8,128)(2,1)}, u32[]{:S(2)}) copy-start(bf16[8,128,1280]{2,1,0:T(8,128)(2,1)} %get-tuple-element.200) | copy-start | bytes 7864324
  961.7 38.1 %copy-start.41 = (f32[1280]{0:T(1024)S(1)}, f32[1280]{0:T(1024)}, u32[]{:S(2)}) copy-start(f32[1280]{0:T(1024)} %get-tuple-element.131) | copy-start | bytes 15364
  999.8 64.8 %copy-start.5 = (f32[8,128,1280]{2,0,1:T(8,128)S(1)}, f32[8,128,1280]{2,0,1:T(8,128)}, u32[]{:S(2)}) copy-start(f32[8,128,1280]{2,0,1:T(8,128)} %bitcast_convert_fusion) | copy-start | bytes 15728644
  999.8 64.8 %copy-start.40 = (f32[1280]{0:T(1024)S(1)}, f32[1280]{0:T(1024)}, u32[]{:S(2)}) copy-start(f32[1280]{0:T(1024)} %get-tuple-element.203) | copy-start | bytes 15364
  999.8 64.8 %copy-start.45 = (bf16[2,1280,1280]{2,1,0:T(8,128)(2,1)S(1)}, bf16[2,1280,1280]{2,1,0:T(8,128)(2,1)}, u32[]{:S(2)}) copy-start(bf16[2,1280,1280]{2,1,0:T(8,128)(2,1)} %param.34) | copy-start | bytes 19660804
  1092.3 22.1 %copy-start.39 = (f32[1280]{0:T(1024)S(1)}, f32[1280]{0:T(1024)}, u32[]{:S(2)}) copy-start(f32[1280]{0:T(1024)} %get-tuple-element.124) | copy-start | bytes 15364
  1093.3 16.7 %collective-permute-start.4 = (bf16[8,1,64,1280]{3,0,2,1:T(8,128)(2,1)S(1)}, bf16[8,1,64,1280]{3,0,2,1:T(8,128)(2,1)S(1)}, u32[]{:S(2)}, u32[]{:S(2)}) collective-permute-start(bf16[8,1,64,1280]{3,0,2,1:T(8,128)(2,1)S(1)} %get-tuple-element.175), channel_id=1, source_target_pairs={{0,1},{1,2},{2,3},{3,4},{4,5},{5,6},{6,7},{8,9},{9,10},{10,11},{11... | collective-permute-start | bytes 3932168 | tf_op jit(solution)/shard_map/ppermute | solution.py:27
  1095.5 19.0 %collective-permute-start.5 = (bf16[8,1,64,1280]{3,0,2,1:T(8,128)(2,1)S(1)}, bf16[8,1,64,1280]{3,0,2,1:T(8,128)(2,1)S(1)}, u32[]{:S(2)}, u32[]{:S(2)}) collective-permute-start(bf16[8,1,64,1280]{3,0,2,1:T(8,128)(2,1)S(1)} %get-tuple-element.176), channel_id=1, source_target_pairs={{1,0},{2,1},{3,2},{4,3},{5,4},{6,5},{7,6},{9,8},{10,9},{11,10},{12... | collective-permute-start | bytes 3932168 | tf_op jit(solution)/shard_map/ppermute | solution.py:28
  1114.4 45.6 %copy-start.17 = (f32[1280]{0:T(1024)S(1)}, f32[1280]{0:T(1024)}, u32[]{:S(2)}) copy-start(f32[1280]{0:T(1024)} %get-tuple-element.113) | copy-start | bytes 15364
  1114.4 45.6 %copy-start.18 = (f32[1280]{0:T(1024)S(1)}, f32[1280]{0:T(1024)}, u32[]{:S(2)}) copy-start(f32[1280]{0:T(1024)} %get-tuple-element.120) | copy-start | bytes 15364
  1160.1 27.1 %slice-start = ((s8[5242880]{0:T(1024)(128)(4,1)}), s8[4194304]{0:T(1024)(128)(4,1)S(1)}, s32[]{:S(2)}) async-start(s8[5242880]{0:T(1024)(128)(4,1)} %bitcast.478), calls=%async_computation.4 | async-start | bytes 8388608
  1160.1 27.1 %slice-start.1 = ((s8[5242880]{0:T(1024)(128)(4,1)}), s8[1048576]{0:T(1024)(128)(4,1)S(1)}, s32[]{:S(2)}) async-start(s8[5242880]{0:T(1024)(128)(4,1)} %bitcast.478), calls=%async_computation.5 | async-start | bytes 2097152
  1160.1 27.1 %copy-start.38 = (f32[1280]{0:T(1024)S(1)}, f32[1280]{0:T(1024)}, u32[]{:S(2)}) copy-start(f32[1280]{0:T(1024)} %get-tuple-element.121) | copy-start | bytes 15364
  1164.0 18.7 %collective-permute-start.6 = (bf16[8,1,64,1280]{3,0,2,1:T(8,128)(2,1)S(1)}, bf16[8,1,64,1280]{3,0,2,1:T(8,128)(2,1)S(1)}, u32[]{:S(2)}, u32[]{:S(2)}) collective-permute-start(bf16[8,1,64,1280]{3,0,2,1:T(8,128)(2,1)S(1)} %get-tuple-element.173), channel_id=1, source_target_pairs={{0,1},{1,2},{2,3},{3,4},{4,5},{5,6},{6,7},{8,9},{9,10},{10,11},{11... | collective-permute-start | bytes 3932168 | tf_op jit(solution)/shard_map/ppermute | solution.py:27
  1168.2 19.0 %collective-permute-start.7 = (bf16[8,1,64,1280]{3,0,2,1:T(8,128)(2,1)S(1)}, bf16[8,1,64,1280]{3,0,2,1:T(8,128)(2,1)S(1)}, u32[]{:S(2)}, u32[]{:S(2)}) collective-permute-start(bf16[8,1,64,1280]{3,0,2,1:T(8,128)(2,1)S(1)} %get-tuple-element.174), channel_id=1, source_target_pairs={{1,0},{2,1},{3,2},{4,3},{5,4},{6,5},{7,6},{9,8},{10,9},{11,10},{12... | collective-permute-start | bytes 3932168 | tf_op jit(solution)/shard_map/ppermute | solution.py:28
  1187.2 36.3 %copy-start.1 = (bf16[8,77,768]{2,0,1:T(8,128)(2,1)S(1)}, bf16[8,77,768]{2,0,1:T(8,128)(2,1)}, u32[]{:S(2)}) copy-start(bf16[8,77,768]{2,0,1:T(8,128)(2,1)} %param.27) | copy-start | bytes 2838532
  (49 other events, 192.2 us)
where the time goes:
time: 1230 us; the launch traced here: 1220 us
  matrix products  594 us (48%)
  waiting for transfers between devices  219 us (18%)
  local copies, waits for them, and re-layouts  162 us (13%)
  blocking collectives  149 us (12%)
  other arithmetic  52.5 us (4%)
  starting transfers between devices  45.3 us (4%)
    conv_general_dilated x4, matrix products, conv_rows(): lax.conv_general_dilated(padded, kernel, (1, 1), ((0, 0), (1, 1)), dimens...  140 us
    dot_general x2, matrix products, transformer_local(): jnp.einsum('bnf,fc->bnc', gated_act, ff_out_w[layer_i], preferred_element...  129 us
    dot_general x34, matrix products, attend_block(): jnp.einsum('bqhd,bkhd->bhqk', q_blk, k_all, preferred_element_type=jnp.fl...  101 us
    all_to_all x1, blocking collectives, transformer_local(): qkv_heads = lax.all_to_all(qkv_loc, 'sp', 3, 2, tiled=True)  91.9 us
    all_to_all x2, waiting for transfers between devices, transformer_local(): att_rows = lax.all_to_all(attended, 'sp', 1, 2, tiled=True)  84.1 us
    dot_general x2, matrix products, transformer_local(): jnp.einsum('bnc,cf->bnf', normed, ff_in_w[layer_i], preferred_element_typ...  76.1 us
    all_to_all x1, waiting for transfers between devices, transformer_local(): qkv_heads = lax.all_to_all(qkv_loc, 'sp', 3, 2, tiled=True)  75.8 us
    psum x5, blocking collectives, group_norm_sp(): total_sums = lax.psum(local_sums, 'sp')  56.8 us
  transfers between devices with their start and end apart: 11, of which 11 were waited for; matrix products, arithmetic and copies ran while one was open for 3% of the time, Pallas kernels for 0%

commit v1 on v0

v1 whole, which is shorter than its diff:
```python
import functools
import math
import jax
import jax.numpy as jnp
from jax import lax
from jax.experimental import pallas as pl
from jax.experimental.pallas import tpu as pltpu
from jax.sharding import PartitionSpec as P

NUM_GROUPS = 32
LANES = 128
VMEM_LIMIT = 60 * 1024 * 1024
LOG2_E = 1.4426950408889634
MESH_ID = pl.DeviceIdType.MESH


def swap_kernel(x_ref, o_ref, *rest, sp_size, with_stats):
    if with_stats:
        stat_ref, send_sems, recv_sems = rest
    else:
        send_sems, recv_sems = rest
    me = lax.axis_index('sp')
    barrier = pltpu.get_barrier_semaphore()
    for step in range(1, sp_size):
        pl.semaphore_signal(barrier, inc=1, device_id={'sp': lax.rem(me + step, sp_size)}, device_id_type=MESH_ID)
    pl.semaphore_wait(barrier, sp_size - 1)
    copies = []
    for step in range(1, sp_size):
        peer = lax.rem(me + step, sp_size)
        copy = pltpu.make_async_remote_copy(
            src_ref=x_ref.at[peer], dst_ref=o_ref.at[me], send_sem=send_sems.at[step], recv_sem=recv_sems.at[step],
            device_id={'sp': peer}, device_id_type=MESH_ID)
        copy.start()
        copies.append(copy)
    own = x_ref[me]
    o_ref[me] = own
    if with_stats:
        vals = own.astype(jnp.float32)
        sums, squares = vals.sum(axis=0, keepdims=True), (vals * vals).sum(axis=0, keepdims=True)
    for step in range(1, sp_size):
        copies[step - 1].wait_recv()
        if with_stats:
            vals = o_ref[lax.rem(me + sp_size - step, sp_size)].astype(jnp.float32)
            sums = sums + vals.sum(axis=0, keepdims=True)
            squares = squares + (vals * vals).sum(axis=0, keepdims=True)
    if with_stats:
        stat_ref[0:1] = sums
        stat_ref[1:2] = squares
    for copy in copies:
        copy.wait_send()


def swap(bands, sp_size, with_stats, collective_id):
    _, tok_n, chan_n = bands.shape
    out_shape = [jax.ShapeDtypeStruct(bands.shape, bands.dtype)]
    if with_stats:
        out_shape.append(jax.ShapeDtypeStruct((2, chan_n), jnp.float32))
    vmem = pl.BlockSpec(memory_space=pltpu.VMEM)
    return pl.pallas_call(
        functools.partial(swap_kernel, sp_size=sp_size, with_stats=with_stats),
        out_shape=out_shape,
        in_specs=[vmem],
        out_specs=[vmem] * len(out_shape),
        scratch_shapes=[pltpu.SemaphoreType.DMA((sp_size,)), pltpu.SemaphoreType.DMA((sp_size,))],
        compiler_params=pltpu.CompilerParams(collective_id=collective_id, has_side_effects=True),
        name='swap',
    )(bands)


def group_affine(sums, squares, count_n, gain, bias, eps_val):
    chan_n = sums.shape[0]
    width = chan_n // NUM_GROUPS
    mean = sums.reshape(NUM_GROUPS, width).sum(axis=1) / count_n
    var = squares.reshape(NUM_GROUPS, width).sum(axis=1) / count_n - mean * mean
    inv_std = lax.rsqrt(var + eps_val)
    return jnp.repeat(mean, width), jnp.repeat(inv_std, width) * gain, bias


def chan_stats(values):
    vals = values.astype(jnp.float32)
    axes = tuple(range(vals.ndim - 1))
    return vals.sum(axis=axes), (vals * vals).sum(axis=axes)


def group_norm(values, stats, gain, bias, eps_val):
    count_n = values.size // NUM_GROUPS
    mean, scale, shift = group_affine(stats[0], stats[1], count_n, gain, bias, eps_val)
    return (values.astype(jnp.float32) - mean) * scale + shift


def conv_bands(act, kernel):
    edge = jnp.zeros_like(act[:1, :1])
    from_above = jnp.concatenate([edge, act[:-1, -1:]], axis=0)
    from_below = jnp.concatenate([act[1:, :1], edge], axis=0)
    padded = jnp.concatenate([from_above, act, from_below], axis=1)
    return lax.conv_general_dilated(padded, kernel, (1, 1), ((0, 0), (1, 1)), dimension_numbers=('NHWC', 'HWIO', 'NHWC'), preferred_element_type=jnp.float32)


def resnet(values, stats, time_row, r, res_norm, res_conv_w, res_conv_b, res_temb_w, res_temb_b):
    first_act = jax.nn.silu(group_norm(values, stats, res_norm[r, 0, 0], res_norm[r, 0, 1], 1e-5)).astype(jnp.bfloat16)
    time_act = jax.nn.silu(time_row.astype(jnp.float32)).astype(jnp.bfloat16)
    time_proj = jnp.dot(time_act, res_temb_w[r], preferred_element_type=jnp.float32)[0] + res_temb_b[r]
    hidden = (conv_bands(first_act, res_conv_w[r, 0]) + res_conv_b[r, 0] + time_proj).astype(jnp.bfloat16)
    second_act = jax.nn.silu(group_norm(hidden, chan_stats(hidden), res_norm[r, 1, 0], res_norm[r, 1, 1], 1e-5)).astype(jnp.bfloat16)
    update = conv_bands(second_act, res_conv_w[r, 1]) + res_conv_b[r, 1]
    return (values.astype(jnp.float32) + update).astype(jnp.bfloat16)


def dot_t(left, right):
    return lax.dot_general(left, right, (((1,), (1,)), ((), ())), preferred_element_type=jnp.float32)


def dot_n(left, right):
    return jnp.dot(left, right, preferred_element_type=jnp.float32)


def layer_norm_rows(values, gain, bias):
    vals = values.astype(jnp.float32)
    vals = vals - vals.mean(axis=-1, keepdims=True)
    var = (vals * vals).mean(axis=-1, keepdims=True)
    return (vals * lax.rsqrt(var + 1e-5) * gain + bias).astype(jnp.bfloat16)


def each_block(tok_n, block, body):
    def step(index, carry):
        body(pl.ds(pl.multiple_of(index * block, block), block))
        return carry
    lax.fori_loop(0, tok_n // block, step, 0)


def head_window(head, dim_n):
    start = head * dim_n
    low = start // LANES * LANES
    high = -(-(start + dim_n) // LANES) * LANES
    return low, high, start - low


def lane_mask(rows_n, width, offset, dim_n):
    lane = lax.broadcasted_iota(jnp.int32, (rows_n, width), 1)
    return (lane >= offset) & (lane < offset + dim_n)


def put_head(o_ref, rows, low, high, offset, dim_n, value):
    if offset:
        lane = lax.broadcasted_iota(jnp.int32, (value.shape[0], LANES), 1)
        o_ref[rows, low:low + LANES] = jnp.where(lane >= offset, value[:, :LANES].astype(jnp.float32), o_ref[rows, low:low + LANES].astype(jnp.float32)).astype(o_ref.dtype)
        o_ref[rows, low + LANES:high] = value[:, LANES:].astype(o_ref.dtype)
    else:
        o_ref[rows, low:high] = value.astype(o_ref.dtype)


def qkv_kernel(u_ref, ln_ref, w_ref, o_ref, n_ref):
    @pl.when(pl.program_id(0) == 0)
    def _():
        def norm(rows):
            n_ref[rows] = layer_norm_rows(u_ref[rows], ln_ref[0, 0:1], ln_ref[0, 1:2])
        each_block(u_ref.shape[0], 64, norm)
    o_ref[...] = dot_t(n_ref[...], w_ref[...]).astype(o_ref.dtype)


def qkv_call(u, ln_par, w, layer, chunk=768):
    tok_n, chan_n = u.shape
    wide = w.shape[1]
    return pl.pallas_call(
        qkv_kernel,
        grid=(wide // chunk,),
        out_shape=jax.ShapeDtypeStruct((tok_n, wide), jnp.bfloat16),
        in_specs=[
            pl.BlockSpec((tok_n, chan_n), lambda j: (0, 0)),
            pl.BlockSpec((None, 3, 2, chan_n), lambda j: (layer, 0, 0, 0)),
            pl.BlockSpec((None, chunk, chan_n), lambda j: (layer, j, 0)),
        ],
        out_specs=pl.BlockSpec((tok_n, chunk), lambda j: (0, j)),
        scratch_shapes=[pltpu.VMEM((tok_n, chan_n), jnp.bfloat16)],
        compiler_params=pltpu.CompilerParams(vmem_limit_bytes=VMEM_LIMIT),
        cost_estimate=pl.CostEstimate(flops=2 * tok_n * chan_n * wide, bytes_accessed=2 * (wide * chan_n + tok_n * chan_n + tok_n * wide), transcendentals=0),
        name='qkv',
    )(u, ln_par, w)


def attend_kernel(q_ref, k_ref, v_ref, o_ref, *, heads, dim_n, block):
    tok_n = q_ref.shape[0]
    scale = LOG2_E / math.sqrt(dim_n)

    def rows_step(rows):
        for head in range(heads):
            low, high, offset = head_window(head, dim_n)
            queries = jnp.where(lane_mask(block, high - low, offset, dim_n), q_ref[rows, low:high], jnp.zeros((), q_ref.dtype))
            scores = dot_t(queries, k_ref[:, low:high])
            top = scores.max(axis=-1, keepdims=True)
            expo = jnp.exp2((scores - top) * scale)
            total = expo.sum(axis=-1, keepdims=True)
            out = dot_n(expo.astype(jnp.bfloat16), v_ref[:, low:high]) * (1.0 / total)
            put_head(o_ref, rows, low, high, offset, dim_n, out)

    each_block(tok_n, block, rows_step)


def attend_call(qkv, head_n, dim_n, block=256):
    tok_n = qkv.shape[0]
    heads = LANES // math.gcd(LANES, dim_n)
    width = heads * dim_n
    groups = head_n // heads
    return pl.pallas_call(
        functools.partial(attend_kernel, heads=heads, dim_n=dim_n, block=block),
        grid=(groups,),
        out_shape=jax.ShapeDtypeStruct((tok_n, head_n * dim_n), jnp.bfloat16),
        in_specs=[
            pl.BlockSpec((tok_n, width), lambda g: (0, g)),
            pl.BlockSpec((tok_n, width), lambda g: (0, groups + g)),
            pl.BlockSpec((tok_n, width), lambda g: (0, 2 * groups + g)),
        ],
        out_specs=pl.BlockSpec((tok_n, width), lambda g: (0, g)),
        compiler_params=pltpu.CompilerParams(vmem_limit_bytes=VMEM_LIMIT),
        cost_estimate=pl.CostEstimate(flops=4 * tok_n * tok_n * head_n * dim_n, bytes_accessed=8 * tok_n * head_n * dim_n, transcendentals=head_n * tok_n * tok_n),
        name='attend',
    )(qkv, qkv, qkv)


def cross_kernel(u_ref, a_ref, ln_ref, wo_ref, bo_ref, wq_ref, k_ref, v_ref, out_ref, q_ref, c_ref, *, head_n, dim_n, key_n):
    carried = (u_ref[...].astype(jnp.float32) + dot_n(a_ref[...], wo_ref[0]) + bo_ref[0:1]).astype(jnp.bfloat16)
    q_ref[...] = dot_t(layer_norm_rows(carried, ln_ref[1, 0:1], ln_ref[1, 1:2]), wq_ref[...]).astype(jnp.bfloat16)
    rows_n = carried.shape[0]
    pad_n = k_ref.shape[0]
    scale = LOG2_E / math.sqrt(dim_n)
    live = lax.broadcasted_iota(jnp.int32, (rows_n, pad_n), 1) < key_n
    for head in range(head_n):
        low, high, offset = head_window(head, dim_n)
        keys = jnp.where(lane_mask(pad_n, high - low, offset, dim_n), k_ref[:, low:high], jnp.zeros((), k_ref.dtype))
        scores = jnp.where(live, dot_t(q_ref[:, low:high], keys), -jnp.inf)
        top = scores.max(axis=-1, keepdims=True)
        expo = jnp.exp2((scores - top) * scale)
        total = expo.sum(axis=-1, keepdims=True)
        out = dot_n(expo.astype(jnp.bfloat16), v_ref[:, low:high]) * (1.0 / total)
        put_head(c_ref, slice(None), low, high, offset, dim_n, out)
    out_ref[...] = (carried.astype(jnp.float32) + dot_n(c_ref[...], wo_ref[1]) + bo_ref[1:2]).astype(jnp.bfloat16)


def cross_call(u, attended, ln_par, attn_out, attn_b, cross_q, kv, layer, head_n, dim_n, key_n, block=256):
    tok_n, chan_n = u.shape
    wide = head_n * dim_n
    pad_n = kv.shape[0]
    return pl.pallas_call(
        functools.partial(cross_kernel, head_n=head_n, dim_n=dim_n, key_n=key_n),
        grid=(tok_n // block,),
        out_shape=jax.ShapeDtypeStruct((tok_n, chan_n), jnp.bfloat16),
        in_specs=[
            pl.BlockSpec((block, chan_n), lambda i: (i, 0)),
            pl.BlockSpec((block, wide), lambda i: (i, 0)),
            pl.BlockSpec((None, 3, 2, chan_n), lambda i: (layer, 0, 0, 0)),
            pl.BlockSpec((None, 2, wide, chan_n), lambda i: (layer, 0, 0, 0)),
            pl.BlockSpec((None, 2, chan_n), lambda i: (layer, 0, 0)),
            pl.BlockSpec((None, wide, chan_n), lambda i: (layer, 0, 0)),
            pl.BlockSpec((pad_n, wide), lambda i: (0, 2 * layer)),
            pl.BlockSpec((pad_n, wide), lambda i: (0, 2 * layer + 1)),
        ],
        out_specs=pl.BlockSpec((block, chan_n), lambda i: (i, 0)),
        scratch_shapes=[pltpu.VMEM((block, wide), jnp.bfloat16), pltpu.VMEM((block, wide), jnp.bfloat16)],
        compiler_params=pltpu.CompilerParams(vmem_limit_bytes=VMEM_LIMIT),
        cost_estimate=pl.CostEstimate(flops=6 * tok_n * chan_n * wide + 4 * tok_n * pad_n * wide, bytes_accessed=6 * wide * chan_n + 6 * tok_n * chan_n, transcendentals=head_n * tok_n * pad_n),
        name='cross',
    )(u, attended, ln_par, attn_out, attn_b, cross_q, kv, kv)


def ff_kernel(u_ref, ln_ref, wa_ref, wb_ref, ba_ref, bb_ref, w2_ref, b2_ref, o_ref, n_ref, acc_ref, *, layer, block):
    step = pl.program_id(0)
    tok_n = u_ref.shape[0]

    @pl.when(step == 0)
    def _():
        def norm(rows):
            n_ref[rows] = layer_norm_rows(u_ref[rows], ln_ref[2, 0:1], ln_ref[2, 1:2])
            acc_ref[rows] = u_ref[rows].astype(jnp.float32) + b2_ref[layer:layer + 1]
        each_block(tok_n, 64, norm)

    def gate(start):
        rows = pl.ds(start, block)
        first = dot_n(n_ref[rows], wa_ref[...]) + ba_ref[layer:layer + 1]
        second = dot_n(n_ref[rows], wb_ref[...]) + bb_ref[layer:layer + 1]
        return (first * (0.5 * second * (1.0 + lax.erf(second * math.sqrt(0.5))))).astype(jnp.bfloat16)

    def add(start, gated):
        rows = pl.ds(start, block)
        acc_ref[rows] += dot_n(gated, w2_ref[...])

    starts = list(range(0, tok_n, block))
    held = gate(starts[0])
    for index, start in enumerate(starts):
        following = gate(starts[index + 1]) if index + 1 < len(starts) else None
        add(start, held)
        held = following

    @pl.when(step == pl.num_programs(0) - 1)
    def _():
        def done(rows):
            o_ref[rows] = acc_ref[rows].astype(o_ref.dtype)
        each_block(tok_n, 64, done)


def ff_call(u, ln_par, ff_in_w, ff_in_b, ff_out_w, ff_out_b, layer, chunk=512, block=256):
    tok_n, chan_n = u.shape
    width = ff_out_w.shape[1]
    steps = width // chunk
    layers = ff_in_b.shape[0]
    return pl.pallas_call(
        functools.partial(ff_kernel, layer=layer, block=block),
        grid=(steps,),
        out_shape=jax.ShapeDtypeStruct((tok_n, chan_n), jnp.bfloat16),
        in_specs=[
            pl.BlockSpec((tok_n, chan_n), lambda j: (0, 0)),
            pl.BlockSpec((None, 3, 2, chan_n), lambda j: (layer, 0, 0, 0)),
            pl.BlockSpec((None, chan_n, chunk), lambda j: (layer, 0, j)),
            pl.BlockSpec((None, chan_n, chunk), lambda j: (layer, 0, steps + j)),
            pl.BlockSpec((layers, chunk), lambda j: (0, j)),
            pl.BlockSpec((layers, chunk), lambda j: (0, steps + j)),
            pl.BlockSpec((None, chunk, chan_n), lambda j: (layer, j, 0)),
            pl.BlockSpec((layers, chan_n), lambda j: (0, 0)),
        ],
        out_specs=pl.BlockSpec((tok_n, chan_n), lambda j: (0, 0)),
        scratch_shapes=[pltpu.VMEM((tok_n, chan_n), jnp.bfloat16), pltpu.VMEM((tok_n, chan_n), jnp.float32)],
        compiler_params=pltpu.CompilerParams(vmem_limit_bytes=VMEM_LIMIT),
        cost_estimate=pl.CostEstimate(flops=6 * tok_n * chan_n * width, bytes_accessed=6 * chan_n * width + 4 * tok_n * chan_n, transcendentals=tok_n * width),
        name='ff',
    )(u, ln_par, ff_in_w, ff_in_w, ff_in_b, ff_in_b, ff_out_w, ff_out_b)


def transformer(hidden, context_row, tr_norm, proj_w, proj_b, ln_par, self_qkv, cross_q, cross_kv, attn_out, attn_b, ff_in_w, ff_in_b, ff_out_w, ff_out_b):
    layers, _, chan_n, head_n, dim_n = self_qkv.shape
    wide = head_n * dim_n
    key_n = context_row.shape[0]
    qkv_w = jnp.transpose(self_qkv, (0, 1, 3, 4, 2)).reshape(layers, 3 * wide, chan_n)
    crq_w = jnp.transpose(cross_q, (0, 2, 3, 1)).reshape(layers, wide, chan_n)
    ckv_w = jnp.transpose(cross_kv, (0, 1, 3, 4, 2)).reshape(layers * 2 * wide, cross_kv.shape[2])
    out_w = attn_out.reshape(layers, 2, wide, chan_n)
    pad_n = -(-key_n // LANES) * LANES
    padded = jnp.pad(context_row, ((0, pad_n - key_n), (0, 0)))
    kv = dot_t(padded, ckv_w).astype(jnp.bfloat16)
    normed = group_norm(hidden, chan_stats(hidden), tr_norm[0], tr_norm[1], 1e-6).astype(jnp.bfloat16)
    u = (dot_n(normed, proj_w[0]) + proj_b[0]).astype(jnp.bfloat16)
    for layer in range(layers):
        qkv = qkv_call(u, ln_par, qkv_w, layer)
        attended = attend_call(qkv, head_n, dim_n)
        u = cross_call(u, attended, ln_par, out_w, attn_b, crq_w, kv, layer, head_n, dim_n, key_n)
        u = ff_call(u, ln_par, ff_in_w, ff_in_b, ff_out_w, ff_out_b, layer)
    return (dot_n(u, proj_w[1]) + proj_b[1] + hidden.astype(jnp.float32)).astype(jnp.bfloat16)


def device_block(latents, time_emb, context, res_norm, res_conv_w, res_conv_b, res_temb_w, res_temb_b, tr_norm, proj_w, proj_b, ln_par, self_qkv, cross_q, cross_kv, attn_out, attn_b, ff_in_w, ff_in_b, ff_out_w, ff_out_b, sp_size):
    batch_n, band_n, cols_n, chan_n = latents.shape
    rows_n = band_n * sp_size
    me = lax.axis_index('sp')
    time_row = lax.dynamic_slice_in_dim(time_emb, me, 1, axis=0)
    context_row = lax.dynamic_index_in_dim(context, me, axis=0, keepdims=False)
    whole, stats = swap(latents.reshape(batch_n, band_n * cols_n, chan_n), sp_size, True, 0)
    values = whole.reshape(sp_size, band_n, cols_n, chan_n)
    first = resnet(values, stats, time_row, 0, res_norm, res_conv_w, res_conv_b, res_temb_w, res_temb_b)
    middle = transformer(first.reshape(rows_n * cols_n, chan_n), context_row, tr_norm, proj_w, proj_b, ln_par, self_qkv, cross_q, cross_kv, attn_out, attn_b, ff_in_w, ff_in_b, ff_out_w, ff_out_b).reshape(values.shape)
    last = resnet(middle, chan_stats(middle), time_row, 1, res_norm, res_conv_w, res_conv_b, res_temb_w, res_temb_b)
    bands = swap(last.reshape(sp_size, band_n * cols_n, chan_n), sp_size, False, 1)[0]
    return bands.reshape(batch_n, band_n, cols_n, chan_n)


def solution(mesh):
    sp_size = mesh.shape['sp']
    row_spec = P('dp', 'sp')
    part_spec = P('dp')
    in_specs = (row_spec, part_spec, part_spec) + (P(),) * 18
    body_fn = functools.partial(device_block, sp_size=sp_size)
    return jax.shard_map(body_fn, mesh=mesh, in_specs=in_specs, out_specs=row_spec, check_vma=False)
```

time: 1230 us -> 522 us (0.42)
  matrix products: 594 us -> 169 us
  Pallas kernels: 0 us -> 299 us
  waiting for transfers between devices: 219 us -> 0 us
  blocking collectives: 149 us -> 0 us
  local copies, waits for them, and re-layouts: 162 us -> 17.5 us
  starting transfers between devices: 45.3 us -> 0 us
  other arithmetic: 52.5 us -> 25.2 us
    dot_general x82 -> x5, matrix products: 454 us -> 25 us  [the longest x2 14.3 us: dot_n(): return jnp.dot(left, right, preferred_element_type=jnp.float32)]
    pallas_call x0 -> x10, Pallas kernels: none -> 299 us  [the longest x2 107 us: ff_call(): pl.pallas_call(functools.partial(ff_kernel, layer=layer, block=block), gr...]
    all_to_all x3 -> x0, waiting for transfers between devices: 160 us -> none  [the longest x2 84.1 us: transformer_local(): att_rows = lax.all_to_all(attended, 'sp', 1, 2, tiled=True)]
    all_to_all x1 -> x0, blocking collectives: 91.9 us -> none  [transformer_local(): qkv_heads = lax.all_to_all(qkv_loc, 'sp', 3, 2, tiled=True)]
    ppermute x8 -> x0, waiting for transfers between devices: 58.6 us -> none  [the longest x4 40.8 us: conv_rows(): from_above = lax.ppermute(act_in[:, -1:], 'sp', to_next)]
    psum x5 -> x0, blocking collectives: 56.8 us -> none  [group_norm_sp(): total_sums = lax.psum(local_sums, 'sp')]
    slice x21 -> x8, local copies, waits for them, and re-layouts: 43.2 us -> 5.33 us  [the longest x4 2.64 us: conv_bands(): from_above = jnp.concatenate([edge, act[:-1, -1:]], axis=0)]
    reduce_sum x51 -> x11, other arithmetic: 33.8 us -> 1.91 us  [the longest x1 0.77 us: chan_stats(): return (vals.sum(axis=axes), (vals * vals).sum(axis=axes))]
  transfers between devices with their start and end apart: 11 -> 0, of which waited for: 11 -> 0; matrix products, arithmetic and copies ran while one was open for 3% -> 0% of each run, Pallas kernels for 0% -> 0%
where the time goes in v1:
time: 522 us; the launch traced here: 512 us
  Pallas kernels  299 us (57%)
  matrix products  169 us (32%)
  other arithmetic  25.2 us (5%)
  local copies, waits for them, and re-layouts  17.5 us (3%)
    conv_general_dilated x4, matrix products, conv_bands(): lax.conv_general_dilated(padded, kernel, (1, 1), ((0, 0), (1, 1)), dimens...  144 us
    pallas_call x2, Pallas kernels, ff_call(): pl.pallas_call(functools.partial(ff_kernel, layer=layer, block=block), gr...  107 us
    pallas_call x2, Pallas kernels, swap(): pl.pallas_call(functools.partial(swap_kernel, sp_size=sp_size, with_stats...  74.1 us
    pallas_call x2, Pallas kernels, cross_call(): pl.pallas_call(functools.partial(cross_kernel, head_n=head_n, dim_n=dim_n...  41.8 us
    pallas_call x2, Pallas kernels, attend_call(): pl.pallas_call(functools.partial(attend_kernel, heads=heads, dim_n=dim_n,...  38.7 us
    pallas_call x2, Pallas kernels, qkv_call(): pl.pallas_call(qkv_kernel, grid=(wide // chunk,), out_shape=jax.ShapeDtyp...  37.3 us
    dot_general x2, matrix products, dot_n(): return jnp.dot(left, right, preferred_element_type=jnp.float32)  14.3 us

profile of v1, /device:TPU:81, one launch (start us, length us, event | category | flops | bytes accessed | tf_op | source)
XLA Modules:
  0.0 512.1 jit_solution(15681433012949417060)
XLA Ops:
  0.0 38.4 %swap.2 = (bf16[8,128,1280]{2,1,0:T(8,128)(2,1)}, f32[2,1280]{1,0:T(2,128)}) custom-call(bf16[8,128,1280]{2,1,0:T(8,128)(2,1)} %bitcast.92), custom_call_target="tpu_custom_call" | custom-call | tf_op jit(solution)/shard_map/swap/pallas_call | solution.py:59
  38.4 0.8 slice_reduce_fusion.14
  39.3 0.1 reduce_sum.162
  39.8 0.8 multiply_reduce_fusion.6
  40.8 2.3 bitcast_convert_fusion
  43.1 3.1 multiply_convert_fusion.1
  46.3 1.7 fusion.138
  48.0 0.2 copy-done.3
  48.1 2.5 fusion.106
  50.7 0.6 slice_reduce_fusion.2
  51.3 0.6 slice_reduce_fusion
  51.9 36.1 %convert_reduce_fusion.1 = (f32[1280]{0:T(1024)S(1)}, f32[1280]{0:T(1024)S(1)}, bf16[8,2,64,1280]{3,0,2,1:T(8,128)(2,1)}) fusion(f32[1280]{0:T(1024)S(1)} %add.215, f32[1280]{0:T(1024)S(1)} %get-tuple-element.27, bf16[2,2,3,3,1280,1280]{5,4,3,2,1,0:T(8,128)(2,1)} %param.25, bf16[7,1,64,1280]{3,0,2,1:T(8,128)(2,1)} %get-tuple-element.44, ...), kind=kOutput, calls=%fused_computation.27 | convolution fusion | flops 29919801344 | bytes 37212160 | tf_op jit(solution)/shard_map/conv_general_dilated | solution.py:96
  88.4 0.1 reduce_sum.167
  88.7 0.8 multiply_reduce_fusion.5
  89.7 3.4 fusion.27
  93.0 0.3 fusion.137
  93.4 0.8 fusion.82.clone.5
  94.1 1.1 slice-done
  95.2 0.4 slice-done.1
  95.6 37.1 %convert_reduce_fusion.2 = (f32[1280]{0:T(1024)S(1)}, f32[1280]{0:T(1024)S(1)}, bf16[8,2,64,1280]{3,0,2,1:T(8,128)(2,1)}) fusion(f32[1280]{0:T(1024)S(1)} %get-tuple-element.26, bf16[2,2,3,3,1280,1280]{5,4,3,2,1,0:T(8,128)(2,1)} %param.25, f32[8,2,64,1280]{3,2,1,0:T(8,128)S(1)} %bitcast.84, bf16[8,4,64,1280]{3,0,2,1:T(8,128)(2,1)S(1)} %fusion.82.clone.5), kind=kOutput, calls=%fused_computation.87 | convolution fusion | flops 29893586944 | bytes 42613760 | tf_op jit(solution)/shard_map/conv_general_dilated | solution.py:96
  133.0 0.1 reduce_sum.171
  133.6 2.6 add_convert_fusion.3
  136.1 0.5 copy.35
  136.7 0.6 slice_reduce_fusion.5
  137.3 6.7 %add_convert_fusion.2.u_ref = bf16[1024,1280]{1,0:T(8,128)(2,1)} fusion(bf16[1024,1280]{1,0:T(8,128)(2,1)S(1)} %bitcast.93, bf16[2,1280,1280]{2,1,0:T(8,128)(2,1)} %param.30, f32[1280]{0:T(1024)S(1)} %get-tuple-element.32), kind=kOutput, calls=%fused_computation.81 | convolution fusion | flops 3358064640 | bytes 8524800 | tf_op jit(solution)/shard_map/dot_general | solution.py:114
  144.0 18.6 %qkv.2.q_ref.k_ref.v_ref = bf16[1024,3840]{1,0:T(8,128)(2,1)} custom-call(bf16[1024,1280]{1,0:T(8,128)(2,1)} %add_convert_fusion.2.u_ref, f32[2,3,2,1280]{3,2,1,0:T(2,128)} %ln_ref.11, bf16[2,3840,1280]{2,1,0:T(8,128)(2,1)} %bitcast.95), custom_call_target="tpu_custom_call" | custom-call | flops 10066329600 | bytes 20316160 | tf_op jit(solution)/shard_map/qkv/pallas_call | solution.py:164
  162.7 19.5 %attend.2.a_ref = bf16[1024,1280]{1,0:T(8,128)(2,1)} custom-call(bf16[1024,3840]{1,0:T(8,128)(2,1)} %qkv.2.q_ref.k_ref.v_ref, bf16[1024,3840]{1,0:T(8,128)(2,1)} %qkv.2.q_ref.k_ref.v_ref, bf16[1024,3840]{1,0:T(8,128)(2,1)} %qkv.2.q_ref.k_ref.v_ref), custom_call_target="tpu_custom_call" | custom-call | flops 5368709120 | bytes 10485760 | tf_op jit(solution)/shard_map/attend/pallas_call | solution.py:204
  182.2 0.2 constant_dynamic-slice_fusion
  182.4 6.9 %convolution_convert_fusion.k_ref.v_ref = bf16[128,5120]{1,0:T(8,128)(2,1)} fusion(bf16[5120,768]{1,0:T(8,128)(2,1)} %bitcast.87, bf16[77,768]{1,0:T(8,128)(2,1)S(1)} %bitcast.94), kind=kOutput, calls=%fused_computation.28 | convolution fusion | flops 1007288320 | bytes 9293312 | tf_op jit(solution)/shard_map/dot_general | solution.py:110
  189.4 20.8 %cross.2.u_ref = bf16[1024,1280]{1,0:T(8,128)(2,1)} custom-call(bf16[1024,1280]{1,0:T(8,128)(2,1)} %add_convert_fusion.2.u_ref, bf16[1024,1280]{1,0:T(8,128)(2,1)} %attend.2.a_ref, f32[2,3,2,1280]{3,2,1,0:T(2,128)} %ln_ref.11, bf16[2,2,1280,1280]{3,2,1,0:T(8,128)(2,1)} %bitcast.97, f32[2,2,1280]{2,1,0:T(2,128)} %bo_ref.3, bf16[2,1280,1280]{2,1,0:T(8,128)(2,1)} %bitcast.99, ...), custom_call_target="tpu_custom_call" | custom-call | flops 10737418240 | bytes 17694720 | tf_op jit(solution)/shard_map/cross/pallas_call | solution.py:243
  210.2 53.6 %ff.2.u_ref = bf16[1024,1280]{1,0:T(8,128)(2,1)} custom-call(bf16[1024,1280]{1,0:T(8,128)(2,1)} %cross.2.u_ref, f32[2,3,2,1280]{3,2,1,0:T(2,128)} %ln_ref.11, bf16[2,1280,10240]{2,1,0:T(8,128)(2,1)} %wb_ref.3, bf16[2,1280,10240]{2,1,0:T(8,128)(2,1)} %wb_ref.3, f32[2,10240]{1,0:T(2,128)} %bb_ref.3, f32[2,10240]{1,0:T(2,128)} %bb_ref.3, ...), custom_call_target="tpu_custom_call" | custom-call | flops 40265318400 | bytes 44564480 | tf_op jit(solution)/shard_map/ff/pallas_call | solution.py:305
  263.8 18.6 %qkv.3.q_ref.k_ref.v_ref = bf16[1024,3840]{1,0:T(8,128)(2,1)} custom-call(bf16[1024,1280]{1,0:T(8,128)(2,1)} %ff.2.u_ref, f32[2,3,2,1280]{3,2,1,0:T(2,128)} %ln_ref.11, bf16[2,3840,1280]{2,1,0:T(8,128)(2,1)} %bitcast.96), custom_call_target="tpu_custom_call" | custom-call | flops 10066329600 | bytes 20316160 | tf_op jit(solution)/shard_map/qkv/pallas_call | solution.py:164
  282.4 19.2 %attend.3.a_ref = bf16[1024,1280]{1,0:T(8,128)(2,1)} custom-call(bf16[1024,3840]{1,0:T(8,128)(2,1)} %qkv.3.q_ref.k_ref.v_ref, bf16[1024,3840]{1,0:T(8,128)(2,1)} %qkv.3.q_ref.k_ref.v_ref, bf16[1024,3840]{1,0:T(8,128)(2,1)} %qkv.3.q_ref.k_ref.v_ref), custom_call_target="tpu_custom_call" | custom-call | flops 5368709120 | bytes 10485760 | tf_op jit(solution)/shard_map/attend/pallas_call | solution.py:204
  301.7 21.0 %cross.3.u_ref = bf16[1024,1280]{1,0:T(8,128)(2,1)} custom-call(bf16[1024,1280]{1,0:T(8,128)(2,1)} %ff.2.u_ref, bf16[1024,1280]{1,0:T(8,128)(2,1)} %attend.3.a_ref, f32[2,3,2,1280]{3,2,1,0:T(2,128)} %ln_ref.11, bf16[2,2,1280,1280]{3,2,1,0:T(8,128)(2,1)} %bitcast.98, f32[2,2,1280]{2,1,0:T(2,128)} %bo_ref.3, bf16[2,1280,1280]{2,1,0:T(8,128)(2,1)} %bitcast.100, ...), custom_call_target="tpu_custom_call" | custom-call | flops 10737418240 | bytes 17694720 | tf_op jit(solution)/shard_map/cross/pallas_call | solution.py:243
  322.7 53.7 %ff.3 = bf16[1024,1280]{1,0:T(8,128)(2,1)} custom-call(bf16[1024,1280]{1,0:T(8,128)(2,1)} %cross.3.u_ref, f32[2,3,2,1280]{3,2,1,0:T(2,128)} %ln_ref.11, bf16[2,1280,10240]{2,1,0:T(8,128)(2,1)} %wb_ref.3, bf16[2,1280,10240]{2,1,0:T(8,128)(2,1)} %wb_ref.3, f32[2,10240]{1,0:T(2,128)} %bb_ref.3, f32[2,10240]{1,0:T(2,128)} %bb_ref.3, ...), custom_call_target="tpu_custom_call" | custom-call | flops 40265318400 | bytes 44564480 | tf_op jit(solution)/shard_map/ff/pallas_call | solution.py:305
  376.4 0.6 copy.37
  377.1 1.1 copy-done.14
  378.2 7.6 %fusion.134 = (f32[1280]{0:T(1024)S(1)}, f32[1280]{0:T(1024)S(1)}, f32[1024,1280]{1,0:T(8,128)}) fusion(f32[8,2,64,1280]{3,2,1,0:T(8,128)S(1)} %copy.37, f32[1280]{0:T(1024)S(1)} %copy-done.11, bf16[1024,1280]{1,0:T(8,128)(2,1)S(1)} %copy-done.14, bf16[2,1280,1280]{2,1,0:T(8,128)(2,1)} %param.30), kind=kOutput, calls=%fused_computation.160 | convolution fusion | flops 3364615680 | bytes 16399360 | tf_op jit(solution)/shard_map/dot_general | solution.py:114
  386.6 6.6 %multiply_convert_fusion = bf16[8,2,64,1280]{3,0,2,1:T(8,128)(2,1)S(1)} fusion(f32[8,2,64,1280]{3,2,1,0:T(8,128)} %bitcast.88, f32[1280]{0:T(1024)S(1)} %get-tuple-element.20, f32[1280]{0:T(1024)S(1)} %get-tuple-element.19, f32[1280]{0:T(1024)S(1)} %sub.78), kind=kLoop, calls=%fused_computation.79 | loop fusion | flops 10485760 | bytes 7879680 | tf_op jit(solution)/shard_map/convert_element_type | solution.py:100
  393.2 0.3 fusion.136
  393.6 1.3 fusion.109
  394.9 35.0 %convert_reduce_fusion = (f32[1280]{0:T(1024)S(1)}, f32[1280]{0:T(1024)S(1)}, bf16[8,2,64,1280]{3,0,2,1:T(8,128)(2,1)}) fusion(f32[1280]{0:T(1024)S(1)} %add.247, f32[1280]{0:T(1024)S(1)} %copy-done.13, bf16[2,2,3,3,1280,1280]{5,4,3,2,1,0:T(8,128)(2,1)} %param.25, bf16[7,1,64,1280]{3,0,2,1:T(8,128)(2,1)S(1)} %get-tuple-element.40, ...), kind=kOutput, calls=%fused_computation.24 | convolution fusion | flops 29919801344 | bytes 37048320 | tf_op jit(solution)/shard_map/conv_general_dilated | solution.py:96
  430.7 3.5 fusion.36
  434.2 0.3 fusion.135
  434.6 35.9 %add_convert_fusion = bf16[8,2,64,1280]{3,0,2,1:T(8,128)(2,1)S(1)} fusion(f32[8,2,64,1280]{3,2,1,0:T(8,128)S(1)} %bitcast.91, bf16[2,2,3,3,1280,1280]{5,4,3,2,1,0:T(8,128)(2,1)} %param.25, bf16[7,1,64,1280]{3,0,2,1:T(8,128)(2,1)S(1)} %get-tuple-element.38, bf16[7,1,64,1280]{3,0,2,1:T(8,128)(2,1)S(1)} %get-tuple-element.37, ...), kind=kOutput, calls=%fused_computation.77 | convolution fusion | flops 29914562560 | bytes 42275840 | tf_op jit(solution)/shard_map/conv_general_dilated | solution.py:96
  470.5 2.0 copy.40
  472.5 35.7 %swap.3 = bf16[8,128,1280]{2,1,0:T(8,128)(2,1)} custom-call(bf16[8,128,1280]{2,1,0:T(8,128)(2,1)} %bitcast.85), custom_call_target="tpu_custom_call" | custom-call | tf_op jit(solution)/shard_map/swap/pallas_call | solution.py:59
  508.2 3.5 copy.49
  (89 shorter events, 3.6 us)
Async XLA Ops:
  0.0 182.2 %copy-start = (bf16[8,77,768]{2,0,1:T(8,128)(2,1)S(1)}, bf16[8,77,768]{2,0,1:T(8,128)(2,1)}, u32[]{:S(2)}) copy-start(bf16[8,77,768]{2,0,1:T(8,128)(2,1)} %param.23) | copy-start | bytes 2838532
  43.1 4.9 copy-start.2
  46.2 1.9 copy-start.3
  46.2 4.4 copy-start.8
  46.2 5.0 copy-start.7
  93.0 2.2 slice-start
  93.4 2.2 slice-start.1
  95.6 37.8 %copy-start.9 = (f32[2,1280]{1,0:T(2,128)S(1)}, f32[2,1280]{1,0:T(2,128)}, u32[]{:S(2)}) copy-start(f32[2,1280]{1,0:T(2,128)} %param.29) | copy-start | bytes 30724
  133.6 3.1 copy-start.10
  322.7 53.7 %copy-start.4 = (bf16[8,2,64,1280]{3,0,2,1:T(8,128)(2,1)S(1)}, bf16[8,2,64,1280]{3,0,2,1:T(8,128)(2,1)}, u32[]{:S(2)}) copy-start(bf16[8,2,64,1280]{3,0,2,1:T(8,128)(2,1)} %get-tuple-element.56) | copy-start | bytes 7864324
  376.4 0.7 copy-start.11
  376.4 1.8 copy-start.14
  378.1 8.2 %copy-start.5 = (f32[2,2,2,1280]{3,2,1,0:T(2,128)S(1)}, f32[2,2,2,1280]{3,2,1,0:T(2,128)}, u32[]{:S(2)}) copy-start(f32[2,2,2,1280]{3,2,1,0:T(2,128)} %param.24) | copy-start | bytes 122884
  386.5 7.0 %slice-start.4 = ((s8[6553600]{0:T(1024)(128)(4,1)}), s8[4194304]{0:T(1024)(128)(4,1)S(1)}, s32[]{:S(2)}) async-start(s8[6553600]{0:T(1024)(128)(4,1)} %bitcast.101), calls=%async_computation.4 | async-start | bytes 8388608
  386.6 7.0 %slice-start.5 = ((s8[6553600]{0:T(1024)(128)(4,1)}), s8[2359296]{0:T(1024)(128)(4,1)S(1)}, s32[]{:S(2)}) async-start(s8[6553600]{0:T(1024)(128)(4,1)} %bitcast.101), calls=%async_computation.5 | async-start | bytes 4718592
  393.2 1.7 copy-start.6
  393.2 1.7 copy-start.13
  430.7 3.9 slice-start.2
  430.7 3.9 slice-start.3
  430.7 3.9 copy-start.12
  472.5 39.2 %copy-start.1 = (bf16[8,77,768]{2,0,1:T(8,128)(2,1)S(1)}, bf16[8,77,768]{2,0,1:T(8,128)(2,1)}, u32[]{:S(2)}) copy-start(bf16[8,77,768]{2,0,1:T(8,128)(2,1)} %param.23) | copy-start | bytes 2838532
